TPU v7x, 256 devices: a whole 4x4x8 slice. The times are simulated.
256 devices in a mesh: bev: 64 (over z, x, core), scene: 4 (over y).
Axes of the slice: x: 4, y: 4, z: 8, core: 2. Of those that a mesh axis runs over, the one named last changes fastest.
Arguments:
- context: bfloat16 [4, 80, 16384], P('scene', None, 'bev'), may hold values from -24 to 24
- depth_logits: float32 [4, 112, 16384], P('scene', None, 'bev'), may hold values from -20 to 300
- send_count: int32 [4, 64, 64], P('scene', 'bev'), may hold values from 0 to 1024, as said below
- slot_point: int32 [4, 64, 64, 1024], P('scene', 'bev'), may hold values from 0 to 28671, as said below
- slot_cell: int32 [4, 64, 64, 1024], P('scene', 'bev'), may hold values from 0 to 255
Outputs:
- bev_features: bfloat16 [16384, 320], P(('bev', 'scene'))
Inputs may be any that keep to these rules, and one draw needn't show every extreme that they name: `send_count`: one entry is 1024 in every pixel block's row. `slot_point`: the live slots of one pixel block name distinct points; slots at or past the count are unused.
All inputs are finite; a program needn't handle non-finite values.
Results may differ from a plain program's by a relative error of at most 0.0062.
Values may be sent and summed in bfloat16 or wider, within the bound.
No kernel may reach another device: no remote copies, remote signals or barrier semaphores. Data moves between devices by JAX's collectives and lax.ppermute only.
A program may use at most 128 MiB of HBM per device.

v0:
```python
import jax
import jax.numpy as jnp
from jax import lax
from jax.sharding import PartitionSpec as P

GRID = 128


def in_blocks(x, dim, devices):
    before, after = (x.shape[:dim], x.shape[dim + 1 :])
    return jnp.moveaxis(x.reshape(*before, devices, -1, *after), dim, 0)


def sum_at_owner(x, axis, dim):
    devices = lax.axis_size(axis)
    tiles = lax.all_to_all(in_blocks(x, dim, devices), axis, 0, 0, tiled=True)
    return jnp.sum(tiles.astype(jnp.float32), axis=0)


def pool_each(values, cell_ids, strip_cells):
    onehot = (
        cell_ids[:, :, None] == jnp.arange(strip_cells, dtype=jnp.int32)[None, None, :]
    ).astype(jnp.bfloat16)
    return jnp.einsum("gcs,gsn->gnc", values, onehot, preferred_element_type=jnp.float32)


def select_points(point_ids, context_map, depth_prob):
    pix_block = context_map.shape[1]
    depth_bins = depth_prob.shape[0]
    depth_bin = point_ids // pix_block
    pixel_ids = point_ids % pix_block
    pixel_hot = (
        pixel_ids[:, :, None] == jnp.arange(pix_block, dtype=jnp.int32)[None, None, :]
    ).astype(jnp.bfloat16)
    depth_hot = (
        depth_bin[:, :, None] == jnp.arange(depth_bins, dtype=jnp.int32)[None, None, :]
    ).astype(jnp.bfloat16)
    features = jnp.einsum("nsp,cp->ncs", pixel_hot, context_map, preferred_element_type=jnp.float32)
    prob_rows = jnp.einsum("nsk,kp->nsp", depth_hot, depth_prob, preferred_element_type=jnp.float32)
    weight = jnp.sum(prob_rows * pixel_hot.astype(jnp.float32), axis=2)
    return (features * weight[:, None, :]).astype(jnp.bfloat16)


def body(context, depth_logits, send_count, slot_point, slot_cell):
    strips = lax.axis_size("bev")
    scenes = lax.axis_size("scene")
    strip_cells = GRID * GRID // strips
    channels = context.shape[1]
    capacity = slot_point.shape[3]
    depth_prob = jax.nn.softmax(depth_logits[0], axis=0).astype(jnp.bfloat16)
    context_map = context[0]
    counts = send_count[0, 0]
    points = slot_point[0, 0]
    live_mask = jnp.arange(capacity, dtype=jnp.int32)[None, :] < counts[:, None]
    targets = jnp.where(live_mask, slot_cell[0, 0], strip_cells)
    values = select_points(points, context_map, depth_prob)
    strip_sum = sum_at_owner(
        pool_each(values, targets, strip_cells)
        .reshape(strip_cells * lax.axis_size("bev"), channels)
        .astype(jnp.bfloat16),
        "bev",
        0,
    )
    quarter = strip_cells // scenes
    rounded = strip_sum.astype(jnp.bfloat16).reshape(scenes, quarter, 1, channels)
    moved = lax.all_to_all(rounded, "scene", split_axis=0, concat_axis=2, tiled=True)
    return moved.reshape(quarter, scenes * channels)


def solution(mesh):
    return jax.shard_map(
        body,
        mesh=mesh,
        in_specs=(
            P("scene", None, "bev"),
            P("scene", None, "bev"),
            P("scene", "bev", None),
            P("scene", "bev", None, None),
            P("scene", "bev", None, None),
        ),
        out_specs=P(("bev", "scene"), None),
        check_vma=False,
    )
```

profile of v0, /device:TPU:2, one launch (start us, length us, event | category | flops | bytes accessed | tf_op | source)
XLA Modules:
  0.0 141.6 jit_solution(11307070710234492354)
XLA Ops:
  0.0 0.0 copy-start
  0.0 0.9 reduce_max.9
  0.9 0.9 fusion.13
  1.9 1.3 add_select_fusion
  3.2 19.7 %multiply_reduce_fusion = f32[64,1024]{1,0:T(8,128)S(1)} fusion(s32[64,1024]{1,0:T(8,128)S(1)} %get-tuple-element.6, s32[64,1024]{1,0:T(8,128)S(1)} %get-tuple-element.5, f32[1,112,256]{2,1,0:T(8,128)} %param.6, f32[256]{0:T(256)S(1)} %fusion.13, f32[256]{0:T(256)S(1)} %reduce_max.9), kind=kOutput, calls=%fused_computation | convolution fusion | flops 3849342976 | bytes 903168 | tf_op jit(solution)/shard_map/nsk,kp->nsp/dot_general | solution.py:39
  22.9 0.0 copy-done
  22.9 15.2 %multiply_convert_fusion.7 = bf16[64,1024,80]{1,2,0:T(8,128)(2,1)S(1)} fusion(f32[64,1024]{1,0:T(8,128)S(1)} %multiply_reduce_fusion, s32[64,1024]{1,0:T(8,128)S(1)} %get-tuple-element.6, bf16[1,80,256]{2,1,0:T(8,128)(2,1)S(1)} %copy-done), kind=kOutput, calls=%fused_computation.10.clone.clone.clone.clone.2 | convolution fusion | flops 2711617536 | bytes 11051008 | tf_op jit(solution)/shard_map/nsp,cp->ncs/dot_general | solution.py:38
  38.1 18.1 %fusion.8 = bf16[64,256,80]{1,2,0:T(8,128)(2,1)S(1)} fusion(s32[64,1024]{1,0:T(8,128)S(1)} %get-tuple-element.7, bf16[64,1024,80]{1,2,0:T(8,128)(2,1)S(1)} %multiply_convert_fusion.7), kind=kOutput, calls=%fused_computation.13 | convolution fusion | flops 2702442496 | bytes 13369344 | tf_op jit(solution)/shard_map/gcs,gsn->gnc/dot_general | solution.py:24
  56.2 74.3 %all_to_all.20 = bf16[64,256,80]{1,2,0:T(8,128)(2,1)S(1)} all-to-all(bf16[64,256,80]{1,2,0:T(8,128)(2,1)S(1)} %fusion.8), channel_id=1, replica_groups=mesh['bev'=64,'scene'=4] {'bev'}, dimensions={0} | all-to-all | bytes 5242880 | tf_op jit(solution)/shard_map/all_to_all | solution.py:16
  130.4 0.4 reduce_sum.32
  130.8 0.1 copy.9
  130.9 9.9 %all_to_all.21 = bf16[4,64,1,80]{3,1,2,0:T(8,128)(2,1)S(1)} all-to-all(bf16[4,64,1,80]{3,1,2,0:T(8,128)(2,1)S(1)} %bitcast.62), channel_id=1, replica_groups=mesh['bev'=64,'scene'=4] {'scene'}, dimensions={0} | all-to-all | bytes 81920 | tf_op jit(solution)/shard_map/all_to_all | solution.py:66
  140.8 0.1 copy.11
  140.9 0.7 reshape.91
Async XLA Ops:
  0.0 22.9 %copy-start = (bf16[1,80,256]{2,1,0:T(8,128)(2,1)S(1)}, bf16[1,80,256]{2,1,0:T(8,128)(2,1)}, u32[]{:S(2)}) copy-start(bf16[1,80,256]{2,1,0:T(8,128)(2,1)} %param.5) | copy-start | bytes 122884
where the time goes:
time: 142 us
  blocking collectives  84.2 us (59%)
  matrix products  53 us (37%)
  other arithmetic  3.52 us (2%)
    all_to_all x1, blocking collectives, sum_at_owner(): tiles = lax.all_to_all(in_blocks(x, dim, devices), axis, 0, 0, tiled=True)  74.3 us
    dot_general x1, matrix products, select_points(): jnp.einsum('nsk,kp->nsp', depth_hot, depth_prob, preferred_element_type=j...  19.7 us
    dot_general x1, matrix products, pool_each(): jnp.einsum('gcs,gsn->gnc', values, onehot, preferred_element_type=jnp.flo...  18.1 us
    dot_general x1, matrix products, select_points(): jnp.einsum('nsp,cp->ncs', pixel_hot, context_map, preferred_element_type=...  15.2 us
    all_to_all x1, blocking collectives, body(): lax.all_to_all(rounded, 'scene', split_axis=0, concat_axis=2, tiled=True)  9.88 us

commit v1 on v0

--- a/solution.py
+++ b/solution.py
@@ -2,8 +2,22 @@
 import jax.numpy as jnp
 from jax import lax
 from jax.sharding import PartitionSpec as P
+from jax.lax import axis_index, axis_size, ppermute
 
 GRID = 128
+
+
+def mark_the_waves(buf):
+    then, piece_now = (axis_size("scene"), axis_index("scene"))
+    latest = buf.shape[0] // then
+    plain = jnp.roll(buf, shift=-piece_now * latest, axis=0)
+    buffers = [lax.slice_in_dim(plain, 0, latest, axis=0)]
+    for p in range(1, then):
+        prior = lax.slice_in_dim(plain, p * latest, (p + 1) * latest, axis=0)
+        buffers.append(ppermute(prior, "scene", [(t, (t + p) % then) for t in range(then)]))
+    state_now = jnp.concatenate(buffers[::-1], 2)
+    step_out = jnp.roll(state_now, (piece_now + 1) * buffers[0].shape[2], 2)
+    return step_out
 
 
 def in_blocks(x, dim, devices):
@@ -63,7 +77,7 @@
     )
     quarter = strip_cells // scenes
     rounded = strip_sum.astype(jnp.bfloat16).reshape(scenes, quarter, 1, channels)
-    moved = lax.all_to_all(rounded, "scene", split_axis=0, concat_axis=2, tiled=True)
+    moved = mark_the_waves(rounded)
     return moved.reshape(quarter, scenes * channels)
 
 

time: 142 us -> 142 us (level)
  blocking collectives: 84.2 us -> 0 us
  waiting for transfers between devices: 0 us -> 65.5 us
  starting transfers between devices: 0 us -> 17.3 us
    all_to_all x2 -> x0, blocking collectives: 84.2 us -> none  [the longest x1 74.3 us: sum_at_owner(): tiles = lax.all_to_all(in_blocks(x, dim, devices), axis, 0, 0, tiled=True)]
    all_to_all x0 -> x1, waiting for transfers between devices: none -> 62.4 us  [sum_at_owner(): tiles = lax.all_to_all(in_blocks(x, dim, devices), axis, 0, 0, tiled=True)]
    all_to_all x0 -> x1, starting transfers between devices: none -> 12 us  [sum_at_owner(): tiles = lax.all_to_all(in_blocks(x, dim, devices), axis, 0, 0, tiled=True)]
    ppermute x0 -> x3, starting transfers between devices: none -> 5.3 us  [mark_the_waves(): ppermute(prior, 'scene', [(t, (t + p) % then) for t in range(then)])]
    ppermute x0 -> x3, waiting for transfers between devices: none -> 3.04 us  [mark_the_waves(): ppermute(prior, 'scene', [(t, (t + p) % then) for t in range(then)])]
  transfers between devices with their start and end apart: 0 -> 4, of which waited for: 0 -> 2; matrix products, arithmetic and copies ran while one was open for 0% -> 0% of each run, Pallas kernels for 0% -> 0%
where the time goes in v1:
time: 142 us; the launch traced here: 141 us
  waiting for transfers between devices  65.5 us (46%)
  matrix products  53.8 us (38%)
  starting transfers between devices  17.3 us (12%)
  other arithmetic  3.57 us (3%)
    all_to_all x1, waiting for transfers between devices, sum_at_owner(): tiles = lax.all_to_all(in_blocks(x, dim, devices), axis, 0, 0, tiled=True)  62.4 us
    dot_general x1, matrix products, select_points(): jnp.einsum('nsk,kp->nsp', depth_hot, depth_prob, preferred_element_type=j...  19.8 us
    dot_general x1, matrix products, pool_each(): jnp.einsum('gcs,gsn->gnc', values, onehot, preferred_element_type=jnp.flo...  18.9 us
    dot_general x1, matrix products, select_points(): jnp.einsum('nsp,cp->ncs', pixel_hot, context_map, preferred_element_type=...  15.2 us
    all_to_all x1, starting transfers between devices, sum_at_owner(): tiles = lax.all_to_all(in_blocks(x, dim, devices), axis, 0, 0, tiled=True)  12 us
    ppermute x3, starting transfers between devices, mark_the_waves(): ppermute(prior, 'scene', [(t, (t + p) % then) for t in range(then)])  5.3 us
    ppermute x3, waiting for transfers between devices, mark_the_waves(): ppermute(prior, 'scene', [(t, (t + p) % then) for t in range(then)])  3.04 us
  transfers between devices with their start and end apart: 4, of which 2 were waited for; matrix products, arithmetic and copies ran while one was open for 0% of the time, Pallas kernels for 0%

profile of v1, /device:TPU:2, one launch (start us, length us, event | category | flops | bytes accessed | tf_op | source)
XLA Modules:
  0.0 141.3 jit_solution(212688974850071946)
XLA Ops:
  0.0 0.0 copy-start
  0.0 0.9 reduce_max.9
  0.9 0.9 fusion.13
  1.9 1.3 add_select_fusion
  3.2 19.8 %multiply_reduce_fusion = f32[64,1024]{1,0:T(8,128)S(1)} fusion(s32[64,1024]{1,0:T(8,128)S(1)} %get-tuple-element.6, s32[64,1024]{1,0:T(8,128)S(1)} %get-tuple-element.5, f32[1,112,256]{2,1,0:T(8,128)} %param.6, f32[256]{0:T(256)S(1)} %fusion.13, f32[256]{0:T(256)S(1)} %reduce_max.9), kind=kOutput, calls=%fused_computation | convolution fusion | flops 3849342976 | bytes 903168 | tf_op jit(solution)/shard_map/nsk,kp->nsp/dot_general | solution.py:53
  22.9 0.0 copy-done
  22.9 15.2 %multiply_convert_fusion.7 = bf16[64,1024,80]{1,2,0:T(8,128)(2,1)S(1)} fusion(f32[64,1024]{1,0:T(8,128)S(1)} %multiply_reduce_fusion, s32[64,1024]{1,0:T(8,128)S(1)} %get-tuple-element.6, bf16[1,80,256]{2,1,0:T(8,128)(2,1)S(1)} %copy-done), kind=kOutput, calls=%fused_computation.10.clone.clone.clone.clone.2 | convolution fusion | flops 2711617536 | bytes 11051008 | tf_op jit(solution)/shard_map/nsp,cp->ncs/dot_general | solution.py:52
  38.1 18.9 %fusion.8 = bf16[64,256,80]{1,2,0:T(8,128)(2,1)} fusion(s32[64,1024]{1,0:T(8,128)S(1)} %get-tuple-element.10, bf16[64,1024,80]{1,2,0:T(8,128)(2,1)S(1)} %multiply_convert_fusion.7), kind=kOutput, calls=%fused_computation.13 | convolution fusion | flops 2702442496 | bytes 13369344 | tf_op jit(solution)/shard_map/gcs,gsn->gnc/dot_general | solution.py:38
  57.0 12.0 %all-to-all-start = ((bf16[64,256,80]{1,2,0:T(8,128)(2,1)}), bf16[64,256,80]{1,2,0:T(8,128)(2,1)S(1)}, u32[]{:S(2)}, u32[]{:S(2)}) async-start(bf16[64,256,80]{1,2,0:T(8,128)(2,1)} %fusion.8), calls=%async_computation | async-start | bytes 5242880 | tf_op jit(solution)/shard_map/all_to_all | solution.py:30
  69.0 62.4 %all-to-all-done = bf16[64,256,80]{1,2,0:T(8,128)(2,1)S(1)} async-done(((bf16[64,256,80]{1,2,0:T(8,128)(2,1)}), bf16[64,256,80]{1,2,0:T(8,128)(2,1)S(1)}, u32[]{:S(2)}, u32[]{:S(2)}) %all-to-all-start) | async-done | bytes 2621472 | tf_op jit(solution)/shard_map/all_to_all | solution.py:30
  131.5 0.4 reduce_sum.32
  131.9 0.1 copy.9
  132.0 0.1 fusion.14
  132.1 3.1 %collective-permute-start = (bf16[1,64,1,80]{3,1,0,2:T(8,128)(2,1)S(1)}, bf16[1,64,1,80]{3,1,0,2:T(8,128)(2,1)S(1)}, u32[]{:S(2)}, u32[]{:S(2)}) collective-permute-start(bf16[1,64,1,80]{3,1,0,2:T(8,128)(2,1)S(1)} %get-tuple-element.9), channel_id=1, source_target_pairs={{0,3},{1,0},{2,1},{3,2},{4,7},{5,4},{6,5},{7,6},{8,11},{9,8},{10,9... | collective-permute-start | bytes 30728 | tf_op jit(solution)/shard_map/ppermute | solution.py:17
  135.2 0.0 collective-permute-start.2
  135.2 2.2 %collective-permute-start.1 = (bf16[1,64,1,80]{3,1,0,2:T(8,128)(2,1)S(1)}, bf16[1,64,1,80]{3,1,0,2:T(8,128)(2,1)S(1)}, u32[]{:S(2)}, u32[]{:S(2)}) collective-permute-start(bf16[1,64,1,80]{3,1,0,2:T(8,128)(2,1)S(1)} %get-tuple-element.8), channel_id=1, source_target_pairs={{0,2},{1,3},{2,0},{3,1},{4,6},{5,7},{6,4},{7,5},{8,10},{9,11},{10,... | collective-permute-start | bytes 30728 | tf_op jit(solution)/shard_map/ppermute | solution.py:17
  137.4 0.0 collective-permute-done
  137.4 3.0 %collective-permute-done.1 = bf16[1,64,1,80]{3,1,0,2:T(8,128)(2,1)S(1)} collective-permute-done((bf16[1,64,1,80]{3,1,0,2:T(8,128)(2,1)S(1)}, bf16[1,64,1,80]{3,1,0,2:T(8,128)(2,1)S(1)}, u32[]{:S(2)}, u32[]{:S(2)}) %collective-permute-start.1) | collective-permute-done | bytes 10272 | tf_op jit(solution)/shard_map/ppermute | solution.py:17
  140.4 0.0 collective-permute-done.2
  140.5 0.1 copy.10
  140.6 0.7 reshape.90
  (10 shorter events, 0.1 us)
Async XLA Ops:
  0.0 22.9 %copy-start = (bf16[1,80,256]{2,1,0:T(8,128)(2,1)S(1)}, bf16[1,80,256]{2,1,0:T(8,128)(2,1)}, u32[]{:S(2)}) copy-start(bf16[1,80,256]{2,1,0:T(8,128)(2,1)} %param.5) | copy-start | bytes 122884
  57.0 74.5 %all-to-all-start = ((bf16[64,256,80]{1,2,0:T(8,128)(2,1)}), bf16[64,256,80]{1,2,0:T(8,128)(2,1)S(1)}, u32[]{:S(2)}, u32[]{:S(2)}) async-start(bf16[64,256,80]{1,2,0:T(8,128)(2,1)} %fusion.8), calls=%async_computation | async-start | bytes 5242880 | tf_op jit(solution)/shard_map/all_to_all | solution.py:30
  132.1 5.3 %collective-permute-start = (bf16[1,64,1,80]{3,1,0,2:T(8,128)(2,1)S(1)}, bf16[1,64,1,80]{3,1,0,2:T(8,128)(2,1)S(1)}, u32[]{:S(2)}, u32[]{:S(2)}) collective-permute-start(bf16[1,64,1,80]{3,1,0,2:T(8,128)(2,1)S(1)} %get-tuple-element.9), channel_id=1, source_target_pairs={{0,3},{1,0},{2,1},{3,2},{4,7},{5,4},{6,5},{7,6},{8,11},{9,8},{10,9... | collective-permute-start | bytes 30728 | tf_op jit(solution)/shard_map/ppermute | solution.py:17
  135.2 5.3 %collective-permute-start.2 = (bf16[1,64,1,80]{3,1,0,2:T(8,128)(2,1)S(1)}, bf16[1,64,1,80]{3,1,0,2:T(8,128)(2,1)S(1)}, u32[]{:S(2)}, u32[]{:S(2)}) collective-permute-start(bf16[1,64,1,80]{3,1,0,2:T(8,128)(2,1)S(1)} %get-tuple-element.7), channel_id=1, source_target_pairs={{0,1},{1,2},{2,3},{3,0},{4,5},{5,6},{6,7},{7,4},{8,9},{9,10},{10,1... | collective-permute-start | bytes 30728 | tf_op jit(solution)/shard_map/ppermute | solution.py:17
  135.2 5.2 %collective-permute-start.1 = (bf16[1,64,1,80]{3,1,0,2:T(8,128)(2,1)S(1)}, bf16[1,64,1,80]{3,1,0,2:T(8,128)(2,1)S(1)}, u32[]{:S(2)}, u32[]{:S(2)}) collective-permute-start(bf16[1,64,1,80]{3,1,0,2:T(8,128)(2,1)S(1)} %get-tuple-element.8), channel_id=1, source_target_pairs={{0,2},{1,3},{2,0},{3,1},{4,6},{5,7},{6,4},{7,5},{8,10},{9,11},{10,... | collective-permute-start | bytes 30728 | tf_op jit(solution)/shard_map/ppermute | solution.py:17
